TPU v7x, 32 devices: a whole 2x2x4 slice. The times are simulated.
32 devices in a mesh: replica: 2 (over x), tp: 16 (over z, y, core).
Axes of the slice: x: 2, y: 2, z: 4, core: 2. Of those that a mesh axis runs over, the one named last changes fastest.
Arguments:
- tokens: bfloat16 [64, 16384], P('replica', 'tp'), parts along dimension 0, may hold values from -90 to 90
- in_gain: bfloat16 [16384], replicated, may hold values from 0.5 to 1.5
- w_query: bfloat16 [16384, 8192], P(None, 'tp'), may hold values from -0.046875 to 0.046875
- w_key: bfloat16 [16384, 1024], P('tp'), may hold values from -0.09375 to 0.09375
- w_value: bfloat16 [16384, 1024], P('tp'), may hold values from -0.046875 to 0.046875
- w_out: bfloat16 [8192, 16384], P('tp'), may hold values from -0.09375 to 0.09375
- cache_keys: bfloat16 [64, 256, 1024], P('replica', 'tp'), parts along dimension 0, may hold values from -910 to 910
- cache_values: bfloat16 [64, 256, 1024], P('replica', 'tp'), parts along dimension 0, may hold values from -24 to 24
- lengths: int32 [64], P('replica'), parts along dimension 0, may hold values from 1 to 255, as said below
- post_gain: bfloat16 [16384], P('tp'), may hold values from 0.5 to 1.5
Outputs:
- hidden: bfloat16 [64, 16384], P('replica', 'tp'), parts along dimension 0
- normed: bfloat16 [64, 16384], P('replica', 'tp'), parts along dimension 0
There are 2 independent parts, one for each index of `replica`. A program takes and returns all parts, laid end to end along the dimension named above; an argument that names none is the same for every part. Nothing has to cross between parts.
Inputs may be any that keep to these rules, and one draw needn't show every extreme that they name: `lengths`: positions already cached for each sequence; in every draw one sequence has exactly 255 and one has 8 or fewer.
All inputs are finite; a program needn't handle non-finite values.
Results may differ from a plain program's by a relative error of at most 0.019.
Values may be sent and summed in bfloat16 or wider, within the bound.
A program may use at most 128 MiB of HBM per device.

v0:
```python
import math
import jax
import jax.numpy as jnp
from jax import lax
from jax.sharding import PartitionSpec as P

HEADS = 64
KVH = 8
HD = 128
epsilon = 1e-05
rotary_base = 500000.0
masked_value = -1e30


def rotate(vectors, positions):
    half_size = vectors.shape[-1] // 2
    exponents = jnp.arange(half_size, dtype=jnp.float32) * (2.0 / vectors.shape[-1])
    frequency = jnp.power(jnp.float32(rotary_base), -exponents)
    angles = positions.astype(jnp.float32)[:, None] * frequency[None, :]
    cosine = jnp.cos(angles)[:, None, :]
    sine_part = jnp.sin(angles)[:, None, :]
    leading = vectors[..., :half_size]
    trailing = vectors[..., half_size:]
    return jnp.concatenate(
        [leading * cosine - trailing * sine_part, trailing * cosine + leading * sine_part], axis=-1
    )


def inverse_rms(rows_wide):
    return lax.rsqrt(jnp.mean(rows_wide * rows_wide, axis=-1, keepdims=True) + epsilon)


def local(
    tokens, in_gain, w_query, w_key, w_value, w_out, cache_keys, cache_values, lengths, post_gain
):
    device_rank = lax.axis_index("tp")
    batch_rows = tokens.shape[0]
    width_dev = tokens.shape[1]
    heads_dev = w_query.shape[1] // HD
    group_size = HEADS // KVH
    positions_dev = cache_keys.shape[1]
    score_scale = 1.0 / math.sqrt(HD)
    gathered = lax.all_gather(tokens, "tp", axis=1, tiled=True)
    residual = gathered.astype(jnp.float32)
    normed_in = (residual * inverse_rms(residual) * in_gain.astype(jnp.float32)).astype(
        jnp.bfloat16
    )
    own_rows = lax.dynamic_slice_in_dim(normed_in, device_rank * width_dev, width_dev, 1)
    key_part = jnp.dot(own_rows, w_key, preferred_element_type=jnp.float32)
    value_part = jnp.dot(own_rows, w_value, preferred_element_type=jnp.float32)
    key_sum, value_sum = lax.psum((key_part, value_part), "tp")
    fresh_key = rotate(key_sum.reshape(batch_rows, KVH, HD), lengths).astype(jnp.bfloat16)
    fresh_value = value_sum.astype(jnp.bfloat16).reshape(batch_rows, KVH, HD)
    query_wide = jnp.dot(normed_in, w_query, preferred_element_type=jnp.float32)
    own_query = rotate(query_wide.reshape(batch_rows, heads_dev, HD), lengths).astype(jnp.bfloat16)
    all_query = lax.all_gather(
        own_query.reshape(batch_rows, heads_dev * HD), "tp", axis=1, tiled=True
    )
    grouped = all_query.reshape(batch_rows, KVH, group_size, HD)
    cached_keys = cache_keys.reshape(batch_rows, positions_dev, KVH, HD)
    cached_values = cache_values.reshape(batch_rows, positions_dev, KVH, HD)
    scores = (
        jnp.einsum("bgqd,bpgd->bgqp", grouped, cached_keys, preferred_element_type=jnp.float32)
        * score_scale
    )
    positions = device_rank * positions_dev + jnp.arange(positions_dev, dtype=jnp.int32)
    visible = (positions[None, :] < lengths[:, None])[:, None, None, :]
    masked = jnp.where(visible, scores, masked_value)
    first_head = device_rank * heads_dev
    shared_head = first_head // group_size
    local_value = lax.dynamic_slice_in_dim(fresh_value, shared_head, 1, 1).astype(jnp.float32)
    fresh_scores = (
        jnp.einsum("bgqd,bgd->bgq", grouped, fresh_key, preferred_element_type=jnp.float32)
        * score_scale
    )
    cache_peak = lax.pmax(jnp.max(masked, axis=-1), "tp")
    overall_all = jnp.maximum(cache_peak, fresh_scores)
    weights = jnp.where(visible, jnp.exp(masked - overall_all[..., None]), 0.0)
    partial_value = jnp.einsum(
        "bgqp,bpgd->bgqd",
        weights.astype(jnp.bfloat16),
        cached_values,
        preferred_element_type=jnp.float32,
    )
    weighted, mass_sum = (
        lax.psum_scatter(
            partial_value.reshape(batch_rows, HEADS, HD), "tp", scatter_dimension=1, tiled=True
        ),
        lax.psum_scatter(
            jnp.sum(weights, axis=-1).reshape(batch_rows, HEADS),
            "tp",
            scatter_dimension=1,
            tiled=True,
        ),
    )
    own_fresh = lax.dynamic_slice_in_dim(
        fresh_scores.reshape(batch_rows, HEADS), first_head, heads_dev, 1
    )
    own_overall = lax.dynamic_slice_in_dim(
        overall_all.reshape(batch_rows, HEADS), first_head, heads_dev, 1
    )
    fresh_weight = jnp.exp(own_fresh - own_overall)
    denominator = mass_sum + fresh_weight
    rounded_fresh = lax.optimization_barrier(fresh_weight.astype(jnp.bfloat16)).astype(jnp.float32)
    weighted = weighted + rounded_fresh[..., None] * local_value
    head_rows = (
        (weighted / denominator[..., None]).astype(jnp.bfloat16).reshape(batch_rows, heads_dev * HD)
    )
    projected = jnp.dot(head_rows, w_out, preferred_element_type=jnp.float32)
    summed = lax.psum(projected, "tp")
    hidden_full = (residual + summed).astype(jnp.bfloat16)
    hidden = lax.dynamic_slice_in_dim(hidden_full, device_rank * width_dev, width_dev, 1)
    row_scale = inverse_rms(hidden_full.astype(jnp.float32))
    normed = (hidden.astype(jnp.float32) * row_scale * post_gain.astype(jnp.float32)).astype(
        jnp.bfloat16
    )
    return (hidden, normed)


def solution(mesh):
    placed = (
        P("replica", "tp"),
        P(),
        P(None, "tp"),
        P("tp", None),
        P("tp", None),
        P("tp", None),
        P("replica", "tp", None),
        P("replica", "tp", None),
        P("replica"),
        P("tp"),
    )
    return jax.shard_map(
        local,
        mesh=mesh,
        in_specs=placed,
        out_specs=(P("replica", "tp"), P("replica", "tp")),
        check_vma=False,
    )
```

profile of v0, /device:TPU:0, one launch (start us, length us, event | category | flops | bytes accessed | tf_op | source)
XLA Modules:
  0.0 332.5 jit_solution(15112100201063493515)
XLA Ops:
  7.2 0.7 all-gather.2.cloned.1.call-update
  8.0 0.8 convert_element_type.51
  8.7 0.7 convert_element_type.53
  9.4 0.7 broadcast_compare_fusion
  10.1 0.1 multiply_cosine_fusion
  10.3 40.5 %all-gather.2.cloned.1.call-done = bf16[32,16384]{1,0:T(8,128)(2,1)} async-done(((bf16[32,1024]{1,0:T(8,128)(2,1)}), bf16[32,16384]{1,0:T(8,128)(2,1)}) %all-gather.2.cloned.1.call-update) | async-done | bytes 1048592 | tf_op jit(solution)/shard_map/all_gather | solution.py:43
  50.8 1.5 fusion
  52.3 1.5 fusion.2
  53.9 0.5 convolution_bitcast_fusion.1
  54.4 0.7 copy.39
  55.1 8.7 %fusion.31 = f32[32,512]{1,0:T(8,128)S(1)} fusion(bf16[32,16384]{1,0:T(8,128)(2,1)S(1)} %fusion.2, bf16[16384,512]{1,0:T(8,128)(2,1)} %param.12), kind=kOutput, calls=%fused_computation.59 | convolution fusion | flops 536870912 | bytes 17891328 | tf_op jit(solution)/shard_map/dot_general | solution.py:54
  64.2 21.0 %all_gather.7 = bf16[32,8192]{1,0:T(8,128)(2,1)S(1)} all-gather(bf16[32,512]{1,0:T(8,128)(2,1)S(1)} %bitcast.62), channel_id=1, replica_groups=mesh['replica'=2,'tp'=16] {'tp'}, dimensions={1}, use_global_device_ids=true | all-gather | bytes 557056 | tf_op jit(solution)/shard_map/all_gather | solution.py:56
  85.3 0.8 copy-done.3
  86.0 0.7 fusion.30
  86.8 58.8 %pmax.7 = f32[32,8,8]{2,1,0:T(8,128)S(1)} all-reduce(f32[32,8,8]{2,1,0:T(8,128)S(1)} %get-tuple-element.18), channel_id=1, replica_groups=mesh['replica'=2,'tp'=16] {'tp'}, use_global_device_ids=true, to_apply=%region_2.0 | all-reduce | flops 2048 | bytes 16384 | tf_op jit(solution)/shard_map/pmax | solution.py:76
  145.6 1.2 subtract_convert_fusion
  146.9 1.4 fusion.15
  148.3 0.7 broadcast_multiply_fusion
  149.0 0.5 convolution_bitcast_fusion
  149.6 1.6 copy.27
  151.3 0.6 dynamic-slice
  152.5 2.1 fusion.17
  154.6 0.7 copy.29
  155.3 0.7 fusion.9
  156.1 59.6 %all-reduce.9 = (f32[32,64]{0,1:T(8,128)S(1)}, bf16[32,1024]{1,0:T(8,128)(2,1)S(1)}) all-reduce(f32[32,64]{0,1:T(8,128)S(1)} %bitcast.60, f32[32,1024]{1,0:T(8,128)S(1)} %fusion.17), channel_id=3, replica_groups=mesh['replica'=2,'tp'=16] {'tp'}, use_global_device_ids=true, to_apply=%region_7.8.clone | all-reduce | flops 34816 | bytes 212992
  215.7 1.0 copy.28
  216.7 0.7 fusion.27
  217.4 10.2 %fusion.20 = f32[32,16384]{1,0:T(8,128)} fusion(bf16[512,16384]{1,0:T(8,128)(2,1)} %param.15, f32[32,4]{0,1:T(4,128)S(1)} %get-tuple-element.15, f32[32,4,128]{2,0,1:T(8,128)} %reduce-scatter.2.cloned.1.call-done, f32[32,128]{1,0:T(8,128)S(1)} %bitcast.59, f32[32,4]{0,1:T(4,128)S(1)} %convert_element_type.57), kind=kOutput, calls=%fused_computation.37 | convolution fusion | flops 536936448 | bytes 18957312 | tf_op jit(solution)/shard_map/dot_general | solution.py:109
  227.7 0.7 copy-done.6
  228.4 94.9 %all-reduce.8.cloned.1.call-done = f32[32,16384]{1,0:T(8,128)} async-done(((f32[32,16384]{1,0:T(8,128)}), f32[32,16384]{1,0:T(8,128)}) %all-reduce.8.cloned.1.call-update) | async-done | bytes 2097168 | tf_op jit(solution)/shard_map/psum | solution.py:110
  323.3 2.0 multiply_reduce_fusion
  325.3 0.7 multiply_convert_fusion
  (38 shorter events, 0.9 us)
Async XLA Ops:
  7.2 46.7 %copy-start = (bf16[1024,1024]{1,0:T(8,128)(2,1)S(1)}, bf16[1024,1024]{1,0:T(8,128)(2,1)}, u32[]{:S(2)}) copy-start(bf16[1024,1024]{1,0:T(8,128)(2,1)} %param.13) | copy-start | bytes 6291460
  7.2 43.6 %all-gather.2.cloned.1.call-start = ((), (), s32[]{:S(2)}) async-start(), calls=%async_computation.1 | async-start | bytes 1114112 | tf_op jit(solution)/shard_map/all_gather | solution.py:43
  7.9 137.7 %all-reduce.6.cloned.1.call-start = ((), (), s32[]{:S(2)}) async-start(), calls=%async_computation.2 | async-start | bytes 262144 | tf_op jit(solution)/shard_map/psum | solution.py:51
  53.9 10.0 %copy-start.2 = (bf16[32,16384]{1,0:T(8,128)(2,1)}, bf16[32,16384]{1,0:T(8,128)(2,1)S(1)}, u32[]{:S(2)}) copy-start(bf16[32,16384]{1,0:T(8,128)(2,1)S(1)} %fusion.2) | copy-start | bytes 3145732
  55.1 162.4 %reduce-scatter.2.cloned.1.call-start = ((), (), s32[]{:S(2)}) async-start(), calls=%async_computation.3 | async-start | bytes 1114112 | tf_op jit(solution)/shard_map/reduce_scatter | solution.py:86
  63.9 22.1 %copy-start.4 = (bf16[32,16,1024]{2,1,0:T(8,128)(2,1)S(1)}, bf16[32,16,1024]{2,1,0:T(8,128)(2,1)}, u32[]{:S(2)}) copy-start(bf16[32,16,1024]{2,1,0:T(8,128)(2,1)} %param.16) | copy-start | bytes 3145732
  85.3 0.8 copy-start.3
  145.6 3.4 %copy-start.5 = (bf16[32,16,1024]{2,1,0:T(8,128)(2,1)S(1)}, bf16[32,16,1024]{2,1,0:T(8,128)(2,1)}, u32[]{:S(2)}) copy-start(bf16[32,16,1024]{2,1,0:T(8,128)(2,1)} %param.17) | copy-start | bytes 3145732
  149.5 1.7 copy-start.7
  151.2 172.1 %all-reduce.8.cloned.1.call-start = ((), (), s32[]{:S(2)}) async-start(), calls=%async_computation.4 | async-start | bytes 4194304 | tf_op jit(solution)/shard_map/psum | solution.py:110
  227.7 0.7 copy-start.6
  227.7 95.6 %copy-start.1 = (bf16[32,16384]{1,0:T(8,128)(2,1)S(1)}, bf16[32,16384]{1,0:T(8,128)(2,1)}, u32[]{:S(2)}) copy-start(bf16[32,16384]{1,0:T(8,128)(2,1)} %all-gather.2.cloned.1.call-done) | copy-start | bytes 3145732
Sparse Core Ops, SparseCore 0:
  10.2 40.5 all-gather.1
  55.2 87.4 all-reduce.5
  151.3 56.5 reduce-scatter.1
  227.8 95.3 all-reduce.7
where the time goes:
time: 333 us
  blocking collectives  139 us (42%)
  waiting for transfers between devices  136 us (41%)
  matrix products  24.2 us (7%)
  between operations  14.6 us (4%)
  other arithmetic  11.6 us (3%)
  local copies, waits for them, and re-layouts  6.35 us (2%)
    psum x1, waiting for transfers between devices, local(): summed = lax.psum(projected, 'tp')  94.9 us
    unnamed x1, blocking collectives  59.6 us
    pmax x1, blocking collectives, local(): cache_peak = lax.pmax(jnp.max(masked, axis=-1), 'tp')  58.8 us
    all_gather x1, waiting for transfers between devices, local(): gathered = lax.all_gather(tokens, 'tp', axis=1, tiled=True)  40.5 us
    all_gather x1, blocking collectives, local(): lax.all_gather(own_query.reshape(batch_rows, heads_dev * HD), 'tp', axis=...  21 us
    dot_general x1, matrix products, local(): projected = jnp.dot(head_rows, w_out, preferred_element_type=jnp.float32)  10.2 us
    dot_general x1, matrix products, local(): query_wide = jnp.dot(normed_in, w_query, preferred_element_type=jnp.float32)  8.74 us
  transfers between devices with their start and end apart: 4, of which 2 were waited for; matrix products, arithmetic and copies ran while one was open for 5% of the time, Pallas kernels for 0%

commit v1 on v0

--- a/solution.py
+++ b/solution.py
@@ -107,7 +107,11 @@
         (weighted / denominator[..., None]).astype(jnp.bfloat16).reshape(batch_rows, heads_dev * HD)
     )
     projected = jnp.dot(head_rows, w_out, preferred_element_type=jnp.float32)
-    summed = lax.psum(projected, "tp")
+    peers = lax.axis_size("tp")
+    summed, reach = (projected, 1)
+    while reach < peers:
+        summed = summed + lax.ppermute(summed, "tp", [(i, i ^ reach) for i in range(peers)])
+        reach = 2 * reach
     hidden_full = (residual + summed).astype(jnp.bfloat16)
     hidden = lax.dynamic_slice_in_dim(hidden_full, device_rank * width_dev, width_dev, 1)
     row_scale = inverse_rms(hidden_full.astype(jnp.float32))

time: 333 us -> 426 us (1.28)
  waiting for transfers between devices: 136 us -> 232 us
    ppermute x0 -> x4, waiting for transfers between devices: none -> 190 us  [local(): lax.ppermute(summed, 'tp', [(i, i ^ reach) for i in range(peers)])]
    psum x1 -> x0, waiting for transfers between devices: 94.9 us -> none  [local(): summed = lax.psum(projected, 'tp')]
  transfers between devices with their start and end apart: 4 -> 7, of which waited for: 2 -> 5; matrix products, arithmetic and copies ran while one was open for 5% -> 4% of each run, Pallas kernels for 0% -> 0%
where the time goes in v1:
time: 426 us; the launch traced here: 425 us
  waiting for transfers between devices  232 us (54%)
  blocking collectives  139 us (33%)
  matrix products  22.9 us (5%)
  between operations  14.7 us (3%)
  other arithmetic  10.9 us (3%)
  local copies, waits for them, and re-layouts  5.72 us (1%)
    ppermute x4, waiting for transfers between devices, local(): lax.ppermute(summed, 'tp', [(i, i ^ reach) for i in range(peers)])  190 us
    unnamed x1, blocking collectives  59.6 us
    pmax x1, blocking collectives, local(): cache_peak = lax.pmax(jnp.max(masked, axis=-1), 'tp')  58.8 us
    all_gather x1, waiting for transfers between devices, local(): gathered = lax.all_gather(tokens, 'tp', axis=1, tiled=True)  40.5 us
    all_gather x1, blocking collectives, local(): lax.all_gather(own_query.reshape(batch_rows, heads_dev * HD), 'tp', axis=...  21 us
    dot_general x1, matrix products, local(): projected = jnp.dot(head_rows, w_out, preferred_element_type=jnp.float32)  8.86 us
    dot_general x1, matrix products, local(): query_wide = jnp.dot(normed_in, w_query, preferred_element_type=jnp.float32)  8.74 us
  transfers between devices with their start and end apart: 7, of which 5 were waited for; matrix products, arithmetic and copies ran while one was open for 4% of the time, Pallas kernels for 0%

profile of v1, /device:TPU:0, one launch (start us, length us, event | category | flops | bytes accessed | tf_op | source)
XLA Modules:
  0.0 425.5 jit_solution(3404575468552198465)
XLA Ops:
  7.2 0.7 all-gather.2.cloned.1.call-update
  8.0 0.8 convert_element_type.51
  8.7 0.7 convert_element_type.53
  9.4 0.7 broadcast_compare_fusion
  10.3 40.5 %all-gather.2.cloned.1.call-done = bf16[32,16384]{1,0:T(8,128)(2,1)} async-done(((bf16[32,1024]{1,0:T(8,128)(2,1)}), bf16[32,16384]{1,0:T(8,128)(2,1)}) %all-gather.2.cloned.1.call-update) | async-done | bytes 1048592 | tf_op jit(solution)/shard_map/all_gather | solution.py:43
  50.8 1.5 fusion
  52.3 1.5 fusion.2
  54.4 0.7 copy.39
  55.1 8.7 %fusion.31 = f32[32,512]{1,0:T(8,128)S(1)} fusion(bf16[32,16384]{1,0:T(8,128)(2,1)S(1)} %fusion.2, bf16[16384,512]{1,0:T(8,128)(2,1)} %param.12), kind=kOutput, calls=%fused_computation.59 | convolution fusion | flops 536870912 | bytes 17891328 | tf_op jit(solution)/shard_map/dot_general | solution.py:54
  64.1 21.0 %all_gather.7 = bf16[32,8192]{1,0:T(8,128)(2,1)S(1)} all-gather(bf16[32,512]{1,0:T(8,128)(2,1)S(1)} %bitcast.62), channel_id=1, replica_groups=mesh['replica'=2,'tp'=16] {'tp'}, dimensions={1}, use_global_device_ids=true | all-gather | bytes 557056 | tf_op jit(solution)/shard_map/all_gather | solution.py:56
  85.3 0.8 copy-done.3
  86.1 0.7 fusion.30
  86.8 58.8 %pmax.7 = f32[32,8,8]{2,1,0:T(8,128)S(1)} all-reduce(f32[32,8,8]{2,1,0:T(8,128)S(1)} %get-tuple-element.18), channel_id=1, replica_groups=mesh['replica'=2,'tp'=16] {'tp'}, use_global_device_ids=true, to_apply=%region_2.0 | all-reduce | flops 2048 | bytes 16384 | tf_op jit(solution)/shard_map/pmax | solution.py:76
  145.6 1.2 subtract_convert_fusion
  146.9 1.4 fusion.15
  148.3 0.7 broadcast_multiply_fusion
  149.0 0.5 convolution_bitcast_fusion
  149.5 1.6 copy.27
  151.2 0.6 dynamic-slice
  152.5 2.1 fusion.17
  154.6 0.7 copy.29
  155.3 0.7 fusion.9
  156.0 59.6 %all-reduce.6 = (f32[32,64]{0,1:T(8,128)S(1)}, bf16[32,1024]{1,0:T(8,128)(2,1)S(1)}) all-reduce(f32[32,64]{0,1:T(8,128)S(1)} %bitcast.60, f32[32,1024]{1,0:T(8,128)S(1)} %fusion.17), channel_id=3, replica_groups=mesh['replica'=2,'tp'=16] {'tp'}, use_global_device_ids=true, to_apply=%region_7.8.clone | all-reduce | flops 34816 | bytes 212992
  215.7 1.0 copy.28
  216.7 0.7 fusion.27
  217.4 8.9 %fusion.20 = f32[32,16384]{1,0:T(8,128)S(1)} fusion(bf16[512,16384]{1,0:T(8,128)(2,1)} %param.15, f32[32,4]{0,1:T(4,128)S(1)} %get-tuple-element.15, f32[32,4,128]{2,0,1:T(8,128)} %reduce-scatter.2.cloned.1.call-done, f32[32,128]{1,0:T(8,128)S(1)} %bitcast.59, f32[32,4]{0,1:T(4,128)S(1)} %convert_element_type.57), kind=kOutput, calls=%fused_computation.37 | convolution fusion | flops 536936448 | bytes 18957312 | tf_op jit(solution)/shard_map/dot_general | solution.py:109
  226.3 4.2 collective-permute-done
  230.7 47.7 %collective-permute-done.1 = f32[32,16384]{1,0:T(8,128)S(1)} collective-permute-done((f32[32,16384]{1,0:T(8,128)S(1)}, f32[32,16384]{1,0:T(8,128)S(1)}, u32[]{:S(2)}, u32[]{:S(2)}) %collective-permute-start.1) | collective-permute-done | bytes 2097184 | tf_op jit(solution)/shard_map/ppermute | solution.py:113
  278.7 46.8 %collective-permute-done.2 = f32[32,16384]{1,0:T(8,128)S(1)} collective-permute-done((f32[32,16384]{1,0:T(8,128)S(1)}, f32[32,16384]{1,0:T(8,128)S(1)}, u32[]{:S(2)}, u32[]{:S(2)}) %collective-permute-start.2) | collective-permute-done | bytes 2097184 | tf_op jit(solution)/shard_map/ppermute | solution.py:113
  326.0 91.8 %collective-permute-done.3 = f32[32,16384]{1,0:T(8,128)S(1)} collective-permute-done((f32[32,16384]{1,0:T(8,128)S(1)}, f32[32,16384]{1,0:T(8,128)S(1)}, u32[]{:S(2)}, u32[]{:S(2)}) %collective-permute-start.3) | collective-permute-done | bytes 2097184 | tf_op jit(solution)/shard_map/ppermute | solution.py:113
  417.7 0.5 multiply_reduce_fusion
  418.2 0.7 multiply_convert_fusion
  (46 shorter events, 2.4 us)
Async XLA Ops:
  7.2 46.7 %copy-start = (bf16[1024,1024]{1,0:T(8,128)(2,1)S(1)}, bf16[1024,1024]{1,0:T(8,128)(2,1)}, u32[]{:S(2)}) copy-start(bf16[1024,1024]{1,0:T(8,128)(2,1)} %param.13) | copy-start | bytes 6291460
  7.2 43.6 %all-gather.2.cloned.1.call-start = ((), (), s32[]{:S(2)}) async-start(), calls=%async_computation.1 | async-start | bytes 1114112 | tf_op jit(solution)/shard_map/all_gather | solution.py:43
  7.9 137.7 %all-reduce.5.cloned.1.call-start = ((), (), s32[]{:S(2)}) async-start(), calls=%async_computation.2 | async-start | bytes 262144 | tf_op jit(solution)/shard_map/psum | solution.py:51
  53.9 10.0 %copy-start.2 = (bf16[32,16384]{1,0:T(8,128)(2,1)}, bf16[32,16384]{1,0:T(8,128)(2,1)S(1)}, u32[]{:S(2)}) copy-start(bf16[32,16384]{1,0:T(8,128)(2,1)S(1)} %fusion.2) | copy-start | bytes 3145732
  55.1 162.4 %reduce-scatter.2.cloned.1.call-start = ((), (), s32[]{:S(2)}) async-start(), calls=%async_computation.3 | async-start | bytes 1114112 | tf_op jit(solution)/shard_map/reduce_scatter | solution.py:86
  63.9 22.2 %copy-start.4 = (bf16[32,16,1024]{2,1,0:T(8,128)(2,1)S(1)}, bf16[32,16,1024]{2,1,0:T(8,128)(2,1)}, u32[]{:S(2)}) copy-start(bf16[32,16,1024]{2,1,0:T(8,128)(2,1)} %param.16) | copy-start | bytes 3145732
  85.2 0.8 copy-start.3
  145.6 3.4 copy-start.5
  149.5 1.7 copy-start.7
  226.3 4.2 collective-permute-start
  230.7 47.7 %collective-permute-start.1 = (f32[32,16384]{1,0:T(8,128)S(1)}, f32[32,16384]{1,0:T(8,128)S(1)}, u32[]{:S(2)}, u32[]{:S(2)}) collective-permute-start(f32[32,16384]{1,0:T(8,128)S(1)} %add.83), channel_id=1, source_target_pairs={{0,2},{1,3},{2,0},{3,1},{4,6},{5,7},{6,4},{7,5},{8,10},{9,11},{10,... | collective-permute-start | bytes 6291464 | tf_op jit(solution)/shard_map/ppermute | solution.py:113
  278.6 47.3 %copy-start.6 = (bf16[1024]{0:T(1024)(128)(2,1)S(1)}, bf16[1024]{0:T(1024)(128)(2,1)}, u32[]{:S(2)}) copy-start(bf16[1024]{0:T(1024)(128)(2,1)} %param.19) | copy-start | bytes 6148
  278.6 139.1 %copy-start.1 = (bf16[32,16384]{1,0:T(8,128)(2,1)S(1)}, bf16[32,16384]{1,0:T(8,128)(2,1)}, u32[]{:S(2)}) copy-start(bf16[32,16384]{1,0:T(8,128)(2,1)} %all-gather.2.cloned.1.call-done) | copy-start | bytes 3145732
  278.6 46.9 %collective-permute-start.2 = (f32[32,16384]{1,0:T(8,128)S(1)}, f32[32,16384]{1,0:T(8,128)S(1)}, u32[]{:S(2)}, u32[]{:S(2)}) collective-permute-start(f32[32,16384]{1,0:T(8,128)S(1)} %add.84), channel_id=1, source_target_pairs={{0,4},{1,5},{2,6},{3,7},{4,0},{5,1},{6,2},{7,3},{8,12},{9,13},{10,... | collective-permute-start | bytes 6291464 | tf_op jit(solution)/shard_map/ppermute | solution.py:113
  325.9 91.9 %collective-permute-start.3 = (f32[32,16384]{1,0:T(8,128)S(1)}, f32[32,16384]{1,0:T(8,128)S(1)}, u32[]{:S(2)}, u32[]{:S(2)}) collective-permute-start(f32[32,16384]{1,0:T(8,128)S(1)} %add.85), channel_id=1, source_target_pairs={{0,8},{1,9},{2,10},{3,11},{4,12},{5,13},{6,14},{7,15},{8,0},{9,1},... | collective-permute-start | bytes 6291464 | tf_op jit(solution)/shard_map/ppermute | solution.py:113
Sparse Core Ops, SparseCore 0:
  10.2 40.5 all-gather.1
  55.2 87.4 all-reduce.4
  151.3 56.6 reduce-scatter.1
